TPU v7x, 32 devices: a whole 2x2x4 slice. The times are simulated.
32 devices in a mesh: rep: 2 (over core), seq: 16 (over z, y, x).
Axes of the slice: x: 2, y: 2, z: 4, core: 2. Of those that a mesh axis runs over, the one named last changes fastest.
Arguments:
- queries: bfloat16 [4096, 8192], P(('rep', 'seq')), parts along dimension 0, may hold values from -180 to 180
- keys: bfloat16 [16384, 1024], P(('rep', 'seq')), parts along dimension 0, may hold values from -6 to 6
- values: bfloat16 [16384, 1024], P(('rep', 'seq')), parts along dimension 0, may hold values from -6 to 6
- vertical: int32 [128, 64], P('rep'), parts along dimension 0, may hold values from 0 to 127, all different within a row
- vert_count: int32 [128], P('rep'), parts along dimension 0, may hold values from 1 to 64
- slash: int32 [128, 32], P('rep'), parts along dimension 0, may hold values from 0 to 95, all different within a row
- slash_count: int32 [128], P('rep'), parts along dimension 0, may hold values from 1 to 32
Outputs:
- attended: bfloat16 [4096, 8192], P(('rep', 'seq')), parts along dimension 0
There are 2 independent parts, one for each index of `rep`. A program takes and returns all parts, laid end to end along the dimension named above; each array names one. Nothing has to cross between parts.
Inputs may be any that keep to these rules, and one draw needn't show every extreme that they name: `vertical`: each row holds 64 different key block numbers; head h uses the first vert_count[h] of them. `slash`: each row holds 32 different numbers; head h uses the first slash_count[h] of them, each number s naming the slash offset s + 1 blocks.
All inputs are finite; a program needn't handle non-finite values.
Results may differ from a plain program's by a relative error of at most 0.007.
Values may be sent and summed in bfloat16 or wider, within the bound.
No kernel may reach another device: no remote copies, remote signals or barrier semaphores. Data moves between devices by JAX's collectives and lax.ppermute only.
A program may use at most 128 MiB of HBM per device.

v0:
```python
import math
import jax
import jax.numpy as jnp
from jax import lax
from jax.sharding import PartitionSpec as P

QUERY_HEADS = 64
KV_HEADS = 8
HEAD_DIM = 128
BLOCK = 64
TURN = 4


def swapped(x, axis, bit):
    return lax.ppermute(x, axis, [(i, i ^ 1 << bit) for i in range(lax.axis_size(axis))])


def absorb(state, scores, valid, combine):
    peak, total, summed = state
    scores = jnp.where(valid, scores, -jnp.inf)
    new_peak = jnp.maximum(peak, jnp.max(scores, axis=1))
    factor = jnp.exp(peak - new_peak)
    weights = jnp.exp(scores - new_peak[:, None])
    total = total * factor + jnp.sum(weights, axis=1)
    summed = summed * factor[:, None] + combine(weights.astype(jnp.bfloat16))
    return (new_peak, total, summed)


def attend(
    query_blocks, storage, slot_of, head, first, stride, vertical, vert_count, slash, slash_count
):
    count_rows, block, width = query_blocks.shape
    total_blocks = storage.shape[0] // block
    cache = storage.reshape(total_blocks, block, 2 * width)
    scale = 1.0 / math.sqrt(width)
    rows = count_rows * block
    absolute = (
        total_blocks
        - count_rows * stride
        + first
        + stride * jnp.arange(count_rows, dtype=jnp.int32)
    )
    verticals = vertical[head]
    live_vert = vert_count[head]
    offsets = slash[head] + 1
    live_slash = slash_count[head]
    lanes = jnp.arange(TURN, dtype=jnp.int32)
    marks = jnp.arange(verticals.shape[0], dtype=jnp.int32) < live_vert
    flat_query = query_blocks.reshape(rows, width)
    diagonal = cache[slot_of(absolute)]
    scores = (
        jnp.einsum(
            "rqd,rkd->rqk", query_blocks, diagonal[:, :, :width], preferred_element_type=jnp.float32
        )
        * scale
    )
    causal = jnp.arange(block)[:, None] >= jnp.arange(block)[None, :]
    scores = jnp.where(causal[None], scores, -jnp.inf)
    peak = jnp.max(scores, axis=2)
    weights = jnp.exp(scores - peak[:, :, None])
    total = jnp.sum(weights, axis=2)
    summed = jnp.einsum(
        "rqk,rkd->rqd",
        weights.astype(jnp.bfloat16),
        diagonal[:, :, width:],
        preferred_element_type=jnp.float32,
    )
    state = (peak.reshape(rows), total.reshape(rows), summed.reshape(rows, width))

    def widen(usable):
        return jnp.broadcast_to(usable[:, None, :, None], (count_rows, block, TURN, block)).reshape(
            rows, TURN * block
        )

    def vertical_turn(step, state):
        picked = lax.dynamic_slice_in_dim(verticals, step * TURN, TURN)
        keys_here = cache[slot_of(picked)].reshape(TURN * block, 2 * width)
        scores = (
            lax.dot_general(
                flat_query,
                keys_here[:, :width],
                (((1,), (1,)), ((), ())),
                preferred_element_type=jnp.float32,
            )
            * scale
        )
        usable = (step * TURN + lanes < live_vert)[None, :] & (picked[None, :] < absolute[:, None])

        def combine(rounded):
            return jnp.dot(rounded, keys_here[:, width:], preferred_element_type=jnp.float32)

        return absorb(state, scores, widen(usable), combine)

    state = lax.fori_loop(0, (live_vert + TURN - 1) // TURN, vertical_turn, state)

    def slash_turn(step, state):
        picked = lax.dynamic_slice_in_dim(offsets, step * TURN, TURN)
        target = absolute[:, None] - picked[None, :]
        keys_here = cache[slot_of(target)].reshape(count_rows, TURN * block, 2 * width)
        scores = (
            jnp.einsum(
                "rqd,rkd->rqk",
                query_blocks,
                keys_here[:, :, :width],
                preferred_element_type=jnp.float32,
            ).reshape(rows, TURN * block)
            * scale
        )
        covered = jnp.any(
            (target[:, :, None] == verticals[None, None, :]) & marks[None, None, :], axis=2
        )
        usable = (step * TURN + lanes < live_slash)[None, :] & jnp.logical_not(covered)

        def combine(rounded):
            return jnp.einsum(
                "rqk,rkd->rqd",
                rounded.reshape(count_rows, block, TURN * block),
                keys_here[:, :, width:],
                preferred_element_type=jnp.float32,
            ).reshape(rows, width)

        return absorb(state, scores, widen(usable), combine)

    state = lax.fori_loop(0, (live_slash + TURN - 1) // TURN, slash_turn, state)
    peak, total, summed = state
    return (summed / total[:, None]).astype(jnp.bfloat16).reshape(count_rows, block, width)


def body(queries, keys, values, vertical, vert_count, slash, slash_count):
    seq_count = lax.axis_size("seq")
    position = lax.axis_index("seq")
    query_rows = queries.shape[0]
    key_rows = keys.shape[0]
    group_devices = seq_count // KV_HEADS
    local_cache = jnp.concatenate(
        [keys.reshape(key_rows, KV_HEADS, HEAD_DIM), values.reshape(key_rows, KV_HEADS, HEAD_DIM)],
        axis=2,
    )
    piece_rows = key_rows // group_devices
    pieces = (
        local_cache.reshape(group_devices, piece_rows, KV_HEADS, 2 * HEAD_DIM)
        .transpose(1, 2, 0, 3)
        .reshape(piece_rows, seq_count, 2 * HEAD_DIM)
    )
    stacked = lax.all_to_all(pieces, "seq", split_axis=1, concat_axis=0, tiled=True).reshape(
        1, seq_count * piece_rows, 2 * HEAD_DIM
    )
    for level in range(group_devices.bit_length() - 1):
        partner = swapped(stacked, "seq", level)
        upper_side = position // 2**level % 2 == 1
        lower = jnp.where(upper_side, partner, stacked)
        upper = jnp.where(upper_side, stacked, partner)
        stacked = jnp.concatenate([lower, upper], axis=0)
    storage = stacked.reshape(group_devices * seq_count * piece_rows, 2 * HEAD_DIM)
    device_blocks = key_rows // BLOCK
    piece_blocks = piece_rows // BLOCK

    def slot_of(index):
        sender = index // device_blocks
        within = index % device_blocks
        return (
            within // piece_blocks * (seq_count * piece_blocks)
            + sender * piece_blocks
            + within % piece_blocks
        )

    per_device = QUERY_HEADS // seq_count
    blocks = queries.reshape(query_rows // BLOCK, BLOCK, QUERY_HEADS, HEAD_DIM)
    gathered = lax.all_to_all(blocks, "seq", split_axis=2, concat_axis=0, tiled=True)
    results = []
    for local in range(per_device):
        results.append(
            attend(
                gathered[:, :, local, :],
                storage,
                slot_of,
                position * per_device + local,
                0,
                1,
                vertical,
                vert_count,
                slash,
                slash_count,
            )
        )
    answer = lax.all_to_all(
        jnp.stack(results, axis=2), "seq", split_axis=0, concat_axis=2, tiled=True
    )
    return answer.reshape(query_rows, QUERY_HEADS * HEAD_DIM)


def solution(mesh):
    return jax.shard_map(
        body,
        mesh=mesh,
        in_specs=(
            P(("rep", "seq"), None),
            P(("rep", "seq"), None),
            P(("rep", "seq"), None),
            P("rep", None),
            P("rep"),
            P("rep", None),
            P("rep"),
        ),
        out_specs=P(("rep", "seq"), None),
        check_vma=False,
    )
```

profile of v0, /device:TPU:0, one launch (start us, length us, event | category | flops | bytes accessed | tf_op | source)
XLA Modules:
  0.0 1188.1 jit_solution(315355499021703888)
XLA Ops:
  3.9 8.3 all-to-all-start
  17.1 38.2 %all-to-all-done = bf16[256,16,256]{2,0,1:T(8,128)(2,1)S(1)} async-done(((bf16[256,16,256]{2,0,1:T(8,128)(2,1)}), bf16[256,16,256]{2,0,1:T(8,128)(2,1)S(1)}, u32[]{:S(2)}, u32[]{:S(2)}) %all-to-all-start) | async-done | bytes 2097184 | tf_op jit(solution)/shard_map/all_to_all | solution.py:145
  56.6 10.0 all-to-all-start.1
  76.7 32.6 %all-to-all-done.1 = bf16[2,64,64,128]{3,1,0,2:T(8,128)(2,1)S(1)} async-done(((bf16[2,64,64,128]{3,1,0,2:T(8,128)(2,1)}), bf16[2,64,64,128]{3,1,0,2:T(8,128)(2,1)S(1)}, u32[]{:S(2)}, u32[]{:S(2)}) %all-to-all-start.1) | async-done | bytes 2097184 | tf_op jit(solution)/shard_map/all_to_all | solution.py:169
  112.2 23.4 %collective-permute-done = bf16[1,4096,256]{2,1,0:T(8,128)(2,1)} collective-permute-done((bf16[1,4096,256]{2,1,0:T(8,128)(2,1)}, bf16[1,4096,256]{2,1,0:T(8,128)(2,1)}, u32[]{:S(2)}, u32[]{:S(2)}) %collective-permute-start) | collective-permute-done | bytes 2097184 | tf_op jit(solution)/shard_map/ppermute | solution.py:15
  155.0 12.7 %while.148 = (s32[]{:T(128)}, f32[2048]{0:T(1024)S(1)}, f32[2048]{0:T(1024)S(1)}, f32[2048,128]{1,0:T(8,128)S(1)}, s32[]{:T(128)}, /*index=5*/s32[]{:T(128)}, s3...) while((s32[]{:T(128)}, f32[2048]{0:T(1024)S(1)}, ...), condition=%wide.region_5.6_spmd.clone, body=%wide.region_2.5_spmd.clone.sunk | while | flops 272635360 | bytes 11539231 | solution.py:94
  157.7 4.2 reshape.1859
  167.7 126.9 %while.152 = (s32[]{:T(128)}, f32[2048]{0:T(1024)S(1)}, f32[2048]{0:T(1024)S(1)}, f32[2048,128]{1,0:T(8,128)S(1)}, s32[]{:T(128)}, /*index=5*/s32[]{:T(128)}, s3...) while((s32[]{:T(128)}, f32[2048]{0:T(1024)S(1)}, ...), condition=%wide.region_10.11_spmd.clone.clone, body=%wide.region_6.10_spmd.clone.clone.sunk | while | flops 274762880 | bytes 32220464 | solution.py:124
  170.1 5.0 gather_fusion
  188.2 5.0 gather_fusion
  206.3 5.0 gather_fusion
  224.5 5.0 gather_fusion
  242.6 5.0 gather_fusion
  260.7 5.0 gather_fusion
  278.8 5.0 gather_fusion
  295.7 195.0 %while.149 = (s32[]{:T(128)}, f32[2048]{0:T(1024)S(1)}, f32[2048]{0:T(1024)S(1)}, f32[2048,128]{1,0:T(8,128)S(1)}, s32[]{:T(128)}, /*index=5*/s32[]{:T(128)}, s3...) while((s32[]{:T(128)}, f32[2048]{0:T(1024)S(1)}, ...), condition=%wide.region_16.17_spmd.clone, body=%wide.region_13.16_spmd.clone.sunk | while | flops 272635360 | bytes 11539231 | solution.py:94
  297.8 4.2 reshape.1862
  310.0 4.2 reshape.1862
  322.2 4.2 reshape.1862
  334.4 4.2 reshape.1862
  346.6 4.2 reshape.1862
  358.8 4.2 reshape.1862
  371.0 4.2 reshape.1862
  383.1 4.2 reshape.1862
  395.3 4.2 reshape.1862
  490.7 125.9 %while.153 = (s32[]{:T(128)}, f32[2048]{0:T(1024)S(1)}, f32[2048]{0:T(1024)S(1)}, f32[2048,128]{1,0:T(8,128)S(1)}, s32[]{:T(128)}, /*index=5*/s32[]{:T(128)}, s3...) while((s32[]{:T(128)}, f32[2048]{0:T(1024)S(1)}, ...), condition=%wide.region_21.22_spmd.clone.clone, body=%wide.region_17.21_spmd.clone.clone.sunk | while | flops 274762880 | bytes 34317640 | solution.py:124
  493.1 5.0 gather_fusion.1
  508.8 5.0 gather_fusion.1
  524.6 5.0 gather_fusion.1
  540.3 5.0 gather_fusion.1
  556.0 5.0 gather_fusion.1
  571.7 5.0 gather_fusion.1
  587.4 5.0 gather_fusion.1
  603.1 5.0 gather_fusion.1
  616.7 81.9 %while.150 = (s32[]{:T(128)}, f32[2048]{0:T(1024)S(1)}, f32[2048]{0:T(1024)S(1)}, f32[2048,128]{1,0:T(8,128)S(1)}, s32[]{:T(128)}, /*index=5*/s32[]{:T(128)}, s3...) while((s32[]{:T(128)}, f32[2048]{0:T(1024)S(1)}, ...), condition=%wide.region_27.28_spmd.clone, body=%wide.region_24.27_spmd.clone.sunk | while | flops 272635360 | bytes 11539231 | solution.py:94
  698.7 126.0 %while.154 = (s32[]{:T(128)}, f32[2048]{0:T(1024)S(1)}, f32[2048]{0:T(1024)S(1)}, f32[2048,128]{1,0:T(8,128)S(1)}, s32[]{:T(128)}, /*index=5*/s32[]{:T(128)}, s3...) while((s32[]{:T(128)}, f32[2048]{0:T(1024)S(1)}, ...), condition=%wide.region_32.33_spmd.clone.clone, body=%wide.region_28.32_spmd.clone.clone.sunk | while | flops 274762880 | bytes 32220464 | solution.py:124
  701.1 5.0 gather_fusion.2
  719.1 5.0 gather_fusion.2
  737.1 5.0 gather_fusion.2
  755.0 5.0 gather_fusion.2
  773.0 5.0 gather_fusion.2
  791.0 5.0 gather_fusion.2
  809.0 5.0 gather_fusion.2
  824.8 61.2 %while.151 = (s32[]{:T(128)}, f32[2048]{0:T(1024)S(1)}, f32[2048]{0:T(1024)S(1)}, f32[2048,128]{1,0:T(8,128)S(1)}, s32[]{:T(128)}, /*index=5*/s32[]{:T(128)}, s3...) while((s32[]{:T(128)}, f32[2048]{0:T(1024)S(1)}, ...), condition=%wide.region_38.39_spmd.clone, body=%wide.region_35.38_spmd.clone.sunk | while | flops 272635360 | bytes 11539231 | solution.py:94
  886.0 35.8 %while.155 = (s32[]{:T(128)}, f32[2048]{0:T(1024)S(1)}, f32[2048]{0:T(1024)S(1)}, f32[2048,128]{1,0:T(8,128)S(1)}, s32[]{:T(128)}, /*index=5*/s32[]{:T(128)}, s3...) while((s32[]{:T(128)}, f32[2048]{0:T(1024)S(1)}, ...), condition=%wide.region_43.44_spmd.clone.clone, body=%wide.region_39.43_spmd.clone.clone.sunk | while | flops 274762880 | bytes 32220464 | solution.py:124
  888.3 5.0 gather_fusion.3
  906.2 5.0 gather_fusion.3
  924.7 258.7 %all_to_all.48 = bf16[32,64,4,128]{3,1,2,0:T(8,128)(2,1)S(1)} all-to-all(bf16[32,64,4,128]{3,1,2,0:T(8,128)(2,1)S(1)} %pad_maximum_fusion.1), channel_id=1, replica_groups=mesh['rep'=2,'seq'=16] {'seq'}, dimensions={0} | all-to-all | bytes 4194304 | tf_op jit(solution)/shard_map/all_to_all | solution.py:186
  (1105 shorter events, 643.5 us)
Async XLA Ops:
  3.9 51.4 %all-to-all-start = ((bf16[256,16,256]{2,0,1:T(8,128)(2,1)}), bf16[256,16,256]{2,0,1:T(8,128)(2,1)S(1)}, u32[]{:S(2)}, u32[]{:S(2)}) async-start(bf16[256,16,256]{2,0,1:T(8,128)(2,1)} %bitcast.1), calls=%async_computation | async-start | bytes 4194304 | tf_op jit(solution)/shard_map/all_to_all | solution.py:145
  17.1 51.5 %copy-start.19 = (s32[64]{0:T(128)S(1)}, s32[64]{0:T(128)}, u32[]{:S(2)}) copy-start(s32[64]{0:T(128)} %param.29) | copy-start | bytes 772
  17.1 51.5 %copy-start.20 = (s32[64]{0:T(128)S(1)}, s32[64]{0:T(128)}, u32[]{:S(2)}) copy-start(s32[64]{0:T(128)} %param.27) | copy-start | bytes 772
  17.1 57.3 %copy-start.16 = (s32[64,32]{0,1:T(8,128)S(1)}, s32[64,32]{0,1:T(8,128)}, u32[]{:S(2)}) copy-start(s32[64,32]{0,1:T(8,128)} %param.28) | copy-start | bytes 24580
  56.6 52.6 %all-to-all-start.1 = ((bf16[2,64,64,128]{3,1,0,2:T(8,128)(2,1)}), bf16[2,64,64,128]{3,1,0,2:T(8,128)(2,1)S(1)}, u32[]{:S(2)}, u32[]{:S(2)}) async-start(bf16[2,64,64,128]{3,1,0,2:T(8,128)(2,1)} %copy.39), calls=%async_computation.1 | async-start | bytes 4194304 | tf_op jit(solution)/shard_map/all_to_all | solution.py:169
  66.7 69.0 %collective-permute-start = (bf16[1,4096,256]{2,1,0:T(8,128)(2,1)}, bf16[1,4096,256]{2,1,0:T(8,128)(2,1)}, u32[]{:S(2)}, u32[]{:S(2)}) collective-permute-start(bf16[1,4096,256]{2,1,0:T(8,128)(2,1)} %bitcast.307), channel_id=1, source_target_pairs={{0,1},{1,0},{2,3},{3,2},{4,5},{5,4},{6,7},{7,6},{8,9},{9,8},{10,11... | collective-permute-start | bytes 6291464 | tf_op jit(solution)/shard_map/ppermute | solution.py:15
  109.4 2.8 copy-start.8
  109.5 26.2 %copy-start.10 = (bf16[256,16,256]{2,0,1:T(8,128)(2,1)S(1)}, bf16[256,16,256]{2,0,1:T(8,128)(2,1)}, u32[]{:S(2)}) copy-start(bf16[256,16,256]{2,0,1:T(8,128)(2,1)} %copy-done.9) | copy-start | bytes 6291460
  142.7 4.6 copy-start.6
  150.4 1.7 copy-start.7
  179.1 4.1 copy-start.2
  197.2 4.1 copy-start.2
  215.3 4.1 copy-start.2
  233.4 4.1 copy-start.2
  251.6 4.1 copy-start.2
  269.7 4.1 copy-start.2
  287.8 4.1 copy-start.2
  493.1 5.0 copy-start.15
  502.1 3.0 copy-start.3
  508.8 5.0 copy-start.15
  517.8 3.0 copy-start.3
  524.6 5.0 copy-start.15
  533.5 3.0 copy-start.3
  540.3 5.0 copy-start.15
  549.2 3.0 copy-start.3
  556.0 5.0 copy-start.15
  564.9 3.0 copy-start.3
  571.7 5.0 copy-start.15
  580.7 3.0 copy-start.3
  587.4 5.0 copy-start.15
  596.4 3.0 copy-start.3
  603.1 5.0 copy-start.15
  612.1 3.0 copy-start.3
  698.6 126.0 %copy-start.17 = (f32[32,64]{1,0:T(8,128)S(1)}, f32[32,64]{1,0:T(8,128)}, u32[]{:S(2)}) copy-start(f32[32,64]{1,0:T(8,128)} %fusion.203) | copy-start | bytes 24580
  698.6 126.1 %copy-start = (f32[32,64,128]{2,1,0:T(8,128)S(1)}, f32[32,64,128]{2,1,0:T(8,128)}, u32[]{:S(2)}) copy-start(f32[32,64,128]{2,1,0:T(8,128)} %fusion.204) | copy-start | bytes 3145732
  698.7 126.1 %copy-start.11 = (f32[2048]{0:T(1024)S(1)}, f32[2048]{0:T(1024)}, u32[]{:S(2)}) copy-start(f32[2048]{0:T(1024)} %reshape.1697) | copy-start | bytes 24580
  698.7 126.1 %copy-start.18 = (s32[1,64]{1,0:T(1,128)S(1)}, s32[1,64]{1,0:T(1,128)}, u32[]{:S(2)}) copy-start(s32[1,64]{1,0:T(1,128)} %get-tuple-element.2841) | copy-start | bytes 772
  710.1 4.0 copy-start.4
  728.0 4.0 copy-start.4
  746.0 4.0 copy-start.4
  764.0 4.0 copy-start.4
  782.0 4.0 copy-start.4
  800.0 4.0 copy-start.4
  818.0 4.0 copy-start.4
  824.8 61.2 %copy-start.21 = (s32[32]{0:T(128)S(1)}, s32[32]{0:T(128)}, u32[]{:S(2)}) copy-start(s32[32]{0:T(128)} %get-tuple-element.2840) | copy-start | bytes 388
  886.0 35.8 %copy-start.13 = (f32[2048]{0:T(1024)S(1)}, f32[2048]{0:T(1024)}, u32[]{:S(2)}) copy-start(f32[2048]{0:T(1024)} %copy-done.12) | copy-start | bytes 24580
  897.2 4.0 copy-start.5
  915.1 4.0 copy-start.5
  (4 other events, 5.1 us)
where the time goes:
time: 1200 us; the launch traced here: 1190 us
  local copies, waits for them, and re-layouts  393 us (33%)
  matrix products  271 us (23%)
  blocking collectives  259 us (22%)
  other arithmetic  139 us (12%)
  waiting for transfers between devices  94.2 us (8%)
  starting transfers between devices  20.3 us (2%)
    all_to_all x1, blocking collectives, body(): lax.all_to_all(jnp.stack(results, axis=2), 'seq', split_axis=0, concat_ax...  259 us
    gather x24, local copies, waits for them, and re-layouts, slash_turn(): cache[slot_of(target)].reshape(count_rows, TURN * block, 2 * width)  120 us
    reshape x30, local copies, waits for them, and re-layouts, widen(): jnp.broadcast_to(usable[:, None, :, None], (count_rows, block, TURN, block))  118 us
    dot_general x24, matrix products, slash_turn(): jnp.einsum('rqd,rkd->rqk', query_blocks, keys_here[:, :, :width], preferr...  91.6 us
    dot_general x24, matrix products, combine(): jnp.einsum('rqk,rkd->rqd', rounded.reshape(count_rows, block, TURN * bloc...  88.2 us
    gather x30, local copies, waits for them, and re-layouts, vertical_turn(): keys_here = cache[slot_of(picked)].reshape(TURN * block, 2 * width)  82.2 us
    dot_general x30, matrix products, vertical_turn(): lax.dot_general(flat_query, keys_here[:, :width], (((1,), (1,)), ((), ())...  51.4 us
    all_to_all x1, waiting for transfers between devices, body(): lax.all_to_all(pieces, 'seq', split_axis=1, concat_axis=0, tiled=True)  38.2 us
  transfers between devices with their start and end apart: 3, of which 3 were waited for; matrix products, arithmetic and copies ran while one was open for 1% of the time, Pallas kernels for 0%

commit v1 on v0

--- a/solution.py
+++ b/solution.py
@@ -183,9 +183,20 @@
                 slash_count,
             )
         )
-    answer = lax.all_to_all(
-        jnp.stack(results, axis=2), "seq", split_axis=0, concat_axis=2, tiled=True
-    )
+    value = jnp.stack(results, axis=2)
+    ways, here = (lax.axis_size("seq"), lax.axis_index("seq"))
+    width_2 = value.shape[0] // ways
+    shape = list(value.shape)
+    shape[0] = width_2
+    height = shape[2]
+    shape[2] = height * ways
+    full = jnp.zeros(shape, value.dtype)
+    for mask in range(ways):
+        part = lax.dynamic_slice_in_dim(value, (here ^ mask) * width_2, width_2, axis=0)
+        if mask:
+            part = lax.ppermute(part, "seq", [(d, d ^ mask) for d in range(ways)])
+        full = lax.dynamic_update_slice_in_dim(full, part, (here ^ mask) * height, axis=2)
+    answer = full
     return answer.reshape(query_rows, QUERY_HEADS * HEAD_DIM)
 
 

time: 1200 us -> 1100 us (0.917)
  blocking collectives: 259 us -> 0 us
  starting transfers between devices: 20.3 us -> 229 us
  local copies, waits for them, and re-layouts: 393 us -> 357 us
  matrix products: 271 us -> 237 us
    all_to_all x1 -> x0, blocking collectives: 259 us -> none  [body(): lax.all_to_all(jnp.stack(results, axis=2), 'seq', split_axis=0, concat_ax...]
    ppermute x0 -> x15, starting transfers between devices: none -> 208 us  [body(): part = lax.ppermute(part, 'seq', [(d, d ^ mask) for d in range(ways)])]
    reshape x30, local copies, waits for them, and re-layouts: 118 us -> 88.7 us  [widen(): jnp.broadcast_to(usable[:, None, :, None], (count_rows, block, TURN, block))]
    broadcast_in_dim x78, local copies, waits for them, and re-layouts: 36.3 us -> 15.9 us  [widen(): jnp.broadcast_to(usable[:, None, :, None], (count_rows, block, TURN, block))]
    dot_general x30, matrix products: 51.4 us -> 35.7 us  [vertical_turn(): lax.dot_general(flat_query, keys_here[:, :width], (((1,), (1,)), ((), ())...]
    ppermute x0 -> x15, waiting for transfers between devices: none -> 15.1 us  [body(): part = lax.ppermute(part, 'seq', [(d, d ^ mask) for d in range(ways)])]
  transfers between devices with their start and end apart: 3 -> 18, of which waited for: 3 -> 9; matrix products, arithmetic and copies ran while one was open for 1% -> 1% of each run, Pallas kernels for 0% -> 0%
where the time goes in v1:
time: 1100 us; the launch traced here: 1080 us
  local copies, waits for them, and re-layouts  357 us (32%)
  matrix products  237 us (22%)
  starting transfers between devices  229 us (21%)
  other arithmetic  140 us (13%)
  waiting for transfers between devices  106 us (10%)
    ppermute x15, starting transfers between devices, body(): part = lax.ppermute(part, 'seq', [(d, d ^ mask) for d in range(ways)])  208 us
    gather x24, local copies, waits for them, and re-layouts, slash_turn(): cache[slot_of(target)].reshape(count_rows, TURN * block, 2 * width)  120 us
    reshape x30, local copies, waits for them, and re-layouts, widen(): jnp.broadcast_to(usable[:, None, :, None], (count_rows, block, TURN, block))  88.7 us
    dot_general x24, matrix products, slash_turn(): jnp.einsum('rqd,rkd->rqk', query_blocks, keys_here[:, :, :width], preferr...  82.7 us
    gather x30, local copies, waits for them, and re-layouts, vertical_turn(): keys_here = cache[slot_of(picked)].reshape(TURN * block, 2 * width)  82.2 us
    dot_general x24, matrix products, combine(): jnp.einsum('rqk,rkd->rqd', rounded.reshape(count_rows, block, TURN * bloc...  80 us
    all_to_all x1, waiting for transfers between devices, body(): lax.all_to_all(pieces, 'seq', split_axis=1, concat_axis=0, tiled=True)  38.2 us
    dot_general x30, matrix products, vertical_turn(): lax.dot_general(flat_query, keys_here[:, :width], (((1,), (1,)), ((), ())...  35.7 us
  transfers between devices with their start and end apart: 18, of which 9 were waited for; matrix products, arithmetic and copies ran while one was open for 1% of the time, Pallas kernels for 0%

profile of v1, /device:TPU:0, one launch (start us, length us, event | category | flops | bytes accessed | tf_op | source)
XLA Modules:
  0.0 1081.3 jit_solution(18215159907768175555)
XLA Ops:
  3.9 8.3 all-to-all-start
  17.1 38.2 %all-to-all-done = bf16[256,16,256]{2,0,1:T(8,128)(2,1)S(1)} async-done(((bf16[256,16,256]{2,0,1:T(8,128)(2,1)}), bf16[256,16,256]{2,0,1:T(8,128)(2,1)S(1)}, u32[]{:S(2)}, u32[]{:S(2)}) %all-to-all-start) | async-done | bytes 2097184 | tf_op jit(solution)/shard_map/all_to_all | solution.py:145
  56.6 10.0 all-to-all-start.1
  76.8 32.4 %all-to-all-done.1 = bf16[2,64,64,128]{3,1,0,2:T(8,128)(2,1)S(1)} async-done(((bf16[2,64,64,128]{3,1,0,2:T(8,128)(2,1)}), bf16[2,64,64,128]{3,1,0,2:T(8,128)(2,1)S(1)}, u32[]{:S(2)}, u32[]{:S(2)}) %all-to-all-start.1) | async-done | bytes 2097184 | tf_op jit(solution)/shard_map/all_to_all | solution.py:169
  115.1 20.6 %collective-permute-done = bf16[1,4096,256]{2,1,0:T(8,128)(2,1)} collective-permute-done((bf16[1,4096,256]{2,1,0:T(8,128)(2,1)}, bf16[1,4096,256]{2,1,0:T(8,128)(2,1)}, u32[]{:S(2)}, u32[]{:S(2)}) %collective-permute-start) | collective-permute-done | bytes 2097184 | tf_op jit(solution)/shard_map/ppermute | solution.py:15
  153.7 12.4 %while.148 = (s32[]{:T(128)}, f32[2048]{0:T(1024)S(1)}, f32[2048]{0:T(1024)S(1)}, f32[2048,128]{1,0:T(8,128)S(1)}, s32[]{:T(128)}, /*index=5*/s32[]{:T(128)}, s3...) while((s32[]{:T(128)}, f32[2048]{0:T(1024)S(1)}, ...), condition=%wide.region_5.6_spmd.clone, body=%wide.region_2.5_spmd.clone.sunk | while | flops 272635360 | bytes 11539231 | solution.py:94
  156.1 4.2 reshape.1858
  166.1 126.2 %while.152 = (s32[]{:T(128)}, f32[2048]{0:T(1024)S(1)}, f32[2048]{0:T(1024)S(1)}, f32[2048,128]{1,0:T(8,128)S(1)}, s32[]{:T(128)}, /*index=5*/s32[]{:T(128)}, s3...) while((s32[]{:T(128)}, f32[2048]{0:T(1024)S(1)}, ...), condition=%wide.region_10.11_spmd.clone.clone, body=%wide.region_6.10_spmd.clone.clone.sunk | while | flops 274762880 | bytes 32220464 | solution.py:124
  168.5 5.0 gather_fusion
  186.5 5.0 gather_fusion
  195.5 4.0 fusion.329
  204.6 5.0 gather_fusion
  213.5 4.0 fusion.329
  222.6 5.0 gather_fusion
  231.6 4.0 fusion.329
  240.6 5.0 gather_fusion
  249.6 4.0 fusion.329
  258.6 5.0 gather_fusion
  267.6 4.0 fusion.329
  276.7 5.0 gather_fusion
  294.8 163.6 %while.149 = (s32[]{:T(128)}, f32[2048]{0:T(1024)S(1)}, f32[2048]{0:T(1024)S(1)}, f32[2048,128]{1,0:T(8,128)S(1)}, s32[]{:T(128)}, /*index=5*/s32[]{:T(128)}, s3...) while((s32[]{:T(128)}, f32[2048]{0:T(1024)S(1)}, ...), condition=%wide.region_16.17_spmd.clone, body=%wide.region_13.16_spmd.clone.sunk | while | flops 272635360 | bytes 11539231 | solution.py:94
  458.4 126.1 %while.153 = (s32[]{:T(128)}, f32[2048]{0:T(1024)S(1)}, f32[2048]{0:T(1024)S(1)}, f32[2048,128]{1,0:T(8,128)S(1)}, s32[]{:T(128)}, /*index=5*/s32[]{:T(128)}, s3...) while((s32[]{:T(128)}, f32[2048]{0:T(1024)S(1)}, ...), condition=%wide.region_21.22_spmd.clone.clone, body=%wide.region_17.21_spmd.clone.clone.sunk | while | flops 274762880 | bytes 34317640 | solution.py:124
  461.0 5.0 gather_fusion.1
  476.8 5.0 gather_fusion.1
  492.5 5.0 gather_fusion.1
  508.2 5.0 gather_fusion.1
  523.9 5.0 gather_fusion.1
  539.6 5.0 gather_fusion.1
  555.3 5.0 gather_fusion.1
  571.0 5.0 gather_fusion.1
  587.0 67.3 %while.150 = (s32[]{:T(128)}, f32[2048]{0:T(1024)S(1)}, f32[2048]{0:T(1024)S(1)}, f32[2048,128]{1,0:T(8,128)S(1)}, s32[]{:T(128)}, /*index=5*/s32[]{:T(128)}, s3...) while((s32[]{:T(128)}, f32[2048]{0:T(1024)S(1)}, ...), condition=%wide.region_27.28_spmd.clone, body=%wide.region_24.27_spmd.clone.sunk | while | flops 272635360 | bytes 11539231 | solution.py:94
  654.3 111.4 %while.154 = (s32[]{:T(128)}, f32[2048]{0:T(1024)S(1)}, f32[2048]{0:T(1024)S(1)}, f32[2048,128]{1,0:T(8,128)S(1)}, s32[]{:T(128)}, /*index=5*/s32[]{:T(128)}, s3...) while((s32[]{:T(128)}, f32[2048]{0:T(1024)S(1)}, ...), condition=%wide.region_32.33_spmd.clone.clone, body=%wide.region_28.32_spmd.clone.clone.sunk | while | flops 274762880 | bytes 23831828 | solution.py:124
  656.6 5.0 gather_fusion.2
  672.5 5.0 gather_fusion.2
  688.4 5.0 gather_fusion.2
  704.4 5.0 gather_fusion.2
  720.3 5.0 gather_fusion.2
  736.2 5.0 gather_fusion.2
  752.1 5.0 gather_fusion.2
  768.2 42.2 %while.151 = (s32[]{:T(128)}, f32[2048]{0:T(1024)S(1)}, f32[2048]{0:T(1024)S(1)}, f32[2048,128]{1,0:T(8,128)S(1)}, s32[]{:T(128)}, /*index=5*/s32[]{:T(128)}, s3...) while((s32[]{:T(128)}, f32[2048]{0:T(1024)S(1)}, ...), condition=%wide.region_38.39_spmd.clone, body=%wide.region_35.38_spmd.clone.sunk | while | flops 272635360 | bytes 11539231 | solution.py:94
  810.5 31.4 %while.155 = (s32[]{:T(128)}, f32[2048]{0:T(1024)S(1)}, f32[2048]{0:T(1024)S(1)}, f32[2048,128]{1,0:T(8,128)S(1)}, s32[]{:T(128)}, /*index=5*/s32[]{:T(128)}, s3...) while((s32[]{:T(128)}, f32[2048]{0:T(1024)S(1)}, ...), condition=%wide.region_43.44_spmd.clone.clone, body=%wide.region_39.43_spmd.clone.clone.sunk | while | flops 274762880 | bytes 34317640 | solution.py:124
  812.7 5.0 gather_fusion.3
  828.4 5.0 gather_fusion.3
  843.8 4.9 pad_maximum_fusion.1
  851.0 12.2 %collective-permute-start.2 = (bf16[2,64,4,128]{3,2,1,0:T(4,128)(2,1)}, bf16[2,64,4,128]{3,2,1,0:T(4,128)(2,1)}, u32[]{:S(2)}, u32[]{:S(2)}) collective-permute-start(bf16[2,64,4,128]{3,2,1,0:T(4,128)(2,1)} %get-tuple-element.2200), channel_id=1, source_target_pairs={{0,2},{1,3},{2,0},{3,1},{4,6},{5,7},{6,4},{7,5},{8,10},{9,11},{10,... | collective-permute-start | bytes 393224 | tf_op jit(solution)/shard_map/ppermute | solution.py:197
  864.7 170.8 %collective-permute-start.4 = (bf16[2,64,4,128]{3,2,1,0:T(4,128)(2,1)}, bf16[2,64,4,128]{3,2,1,0:T(4,128)(2,1)S(1)}, u32[]{:S(2)}, u32[]{:S(2)}) collective-permute-start(bf16[2,64,4,128]{3,2,1,0:T(4,128)(2,1)} %get-tuple-element.2198), channel_id=1, source_target_pairs={{0,4},{1,5},{2,6},{3,7},{4,0},{5,1},{6,2},{7,3},{8,12},{9,13},{10,... | collective-permute-start | bytes 393224 | tf_op jit(solution)/shard_map/ppermute | solution.py:197
  1052.7 6.9 collective-permute-done.8
  1059.6 5.2 collective-permute-start.13
  (1150 shorter events, 615.6 us)
Async XLA Ops:
  3.9 51.4 %all-to-all-start = ((bf16[256,16,256]{2,0,1:T(8,128)(2,1)}), bf16[256,16,256]{2,0,1:T(8,128)(2,1)S(1)}, u32[]{:S(2)}, u32[]{:S(2)}) async-start(bf16[256,16,256]{2,0,1:T(8,128)(2,1)} %bitcast.1), calls=%async_computation | async-start | bytes 4194304 | tf_op jit(solution)/shard_map/all_to_all | solution.py:145
  17.1 51.5 %copy-start.22 = (s32[64]{0:T(128)S(1)}, s32[64]{0:T(128)}, u32[]{:S(2)}) copy-start(s32[64]{0:T(128)} %param.29) | copy-start | bytes 772
  17.1 51.5 %copy-start.23 = (s32[64]{0:T(128)S(1)}, s32[64]{0:T(128)}, u32[]{:S(2)}) copy-start(s32[64]{0:T(128)} %param.27) | copy-start | bytes 772
  17.1 57.4 %copy-start.19 = (s32[64,32]{0,1:T(8,128)S(1)}, s32[64,32]{0,1:T(8,128)}, u32[]{:S(2)}) copy-start(s32[64,32]{0,1:T(8,128)} %param.28) | copy-start | bytes 24580
  56.6 52.6 %all-to-all-start.1 = ((bf16[2,64,64,128]{3,1,0,2:T(8,128)(2,1)}), bf16[2,64,64,128]{3,1,0,2:T(8,128)(2,1)S(1)}, u32[]{:S(2)}, u32[]{:S(2)}) async-start(bf16[2,64,64,128]{3,1,0,2:T(8,128)(2,1)} %copy.53), calls=%async_computation.1 | async-start | bytes 4194304 | tf_op jit(solution)/shard_map/all_to_all | solution.py:169
  66.7 69.0 %collective-permute-start = (bf16[1,4096,256]{2,1,0:T(8,128)(2,1)}, bf16[1,4096,256]{2,1,0:T(8,128)(2,1)}, u32[]{:S(2)}, u32[]{:S(2)}) collective-permute-start(bf16[1,4096,256]{2,1,0:T(8,128)(2,1)} %bitcast.309), channel_id=1, source_target_pairs={{0,1},{1,0},{2,3},{3,2},{4,5},{5,4},{6,7},{7,6},{8,9},{9,8},{10,11... | collective-permute-start | bytes 6291464 | tf_op jit(solution)/shard_map/ppermute | solution.py:15
  112.4 30.3 %copy-start.8 = (bf16[16,2,64,4,128]{4,2,1,0,3:T(8,128)(2,1)}, bf16[16,2,64,4,128]{4,2,1,0,3:T(8,128)(2,1)S(1)}, u32[]{:S(2)}) copy-start(bf16[16,2,64,4,128]{4,2,1,0,3:T(8,128)(2,1)S(1)} %copy.55) | copy-start | bytes 6291460
  112.4 23.3 %copy-start.11 = (bf16[256,16,256]{2,0,1:T(8,128)(2,1)S(1)}, bf16[256,16,256]{2,0,1:T(8,128)(2,1)}, u32[]{:S(2)}) copy-start(bf16[256,16,256]{2,0,1:T(8,128)(2,1)} %copy-done.10) | copy-start | bytes 6291460
  142.7 3.2 copy-start.6
  177.5 4.0 copy-start.1
  195.5 4.0 copy-start.1
  213.5 4.0 copy-start.1
  231.6 4.0 copy-start.1
  249.6 4.0 copy-start.1
  267.6 4.0 copy-start.1
  285.6 4.0 copy-start.1
  461.0 5.0 copy-start.18
  470.0 3.0 copy-start.2
  476.7 5.0 copy-start.18
  485.7 3.0 copy-start.2
  492.5 5.0 copy-start.18
  508.2 5.0 copy-start.18
  523.9 5.0 copy-start.18
  532.8 3.0 copy-start.2
  539.6 5.0 copy-start.18
  548.6 3.0 copy-start.2
  555.3 5.0 copy-start.18
  571.0 5.0 copy-start.18
  768.2 42.2 %copy-start.24 = (s32[32]{0:T(128)S(1)}, s32[32]{0:T(128)}, u32[]{:S(2)}) copy-start(s32[32]{0:T(128)} %get-tuple-element.2856) | copy-start | bytes 388
  812.7 5.0 copy-start.17
  821.7 3.0 copy-start.3
  828.4 5.0 copy-start.17
  837.4 3.0 copy-start.3
  851.0 185.4 %collective-permute-start.1 = (bf16[2,64,4,128]{3,2,1,0:T(4,128)(2,1)}, bf16[2,64,4,128]{3,2,1,0:T(4,128)(2,1)}, u32[]{:S(2)}, u32[]{:S(2)}) collective-permute-start(bf16[2,64,4,128]{3,2,1,0:T(4,128)(2,1)} %get-tuple-element.2201), channel_id=1, source_target_pairs={{0,1},{1,0},{2,3},{3,2},{4,5},{5,4},{6,7},{7,6},{8,9},{9,8},{10,11... | collective-permute-start | bytes 393224 | tf_op jit(solution)/shard_map/ppermute | solution.py:197
  851.0 189.9 %collective-permute-start.2 = (bf16[2,64,4,128]{3,2,1,0:T(4,128)(2,1)}, bf16[2,64,4,128]{3,2,1,0:T(4,128)(2,1)}, u32[]{:S(2)}, u32[]{:S(2)}) collective-permute-start(bf16[2,64,4,128]{3,2,1,0:T(4,128)(2,1)} %get-tuple-element.2200), channel_id=1, source_target_pairs={{0,2},{1,3},{2,0},{3,1},{4,6},{5,7},{6,4},{7,5},{8,10},{9,11},{10,... | collective-permute-start | bytes 393224 | tf_op jit(solution)/shard_map/ppermute | solution.py:197
  863.2 179.4 %collective-permute-start.3 = (bf16[2,64,4,128]{3,2,1,0:T(4,128)(2,1)}, bf16[2,64,4,128]{3,2,1,0:T(4,128)(2,1)S(1)}, u32[]{:S(2)}, u32[]{:S(2)}) collective-permute-start(bf16[2,64,4,128]{3,2,1,0:T(4,128)(2,1)} %get-tuple-element.2199), channel_id=1, source_target_pairs={{0,3},{1,2},{2,1},{3,0},{4,7},{5,6},{6,5},{7,4},{8,11},{9,10},{10,... | collective-permute-start | bytes 393224 | tf_op jit(solution)/shard_map/ppermute | solution.py:197
  864.7 178.2 %collective-permute-start.4 = (bf16[2,64,4,128]{3,2,1,0:T(4,128)(2,1)}, bf16[2,64,4,128]{3,2,1,0:T(4,128)(2,1)S(1)}, u32[]{:S(2)}, u32[]{:S(2)}) collective-permute-start(bf16[2,64,4,128]{3,2,1,0:T(4,128)(2,1)} %get-tuple-element.2198), channel_id=1, source_target_pairs={{0,4},{1,5},{2,6},{3,7},{4,0},{5,1},{6,2},{7,3},{8,12},{9,13},{10,... | collective-permute-start | bytes 393224 | tf_op jit(solution)/shard_map/ppermute | solution.py:197
  1035.5 11.0 %collective-permute-start.5 = (bf16[2,64,4,128]{3,2,1,0:T(4,128)(2,1)S(1)}, bf16[2,64,4,128]{3,2,1,0:T(4,128)(2,1)S(1)}, u32[]{:S(2)}, u32[]{:S(2)}) collective-permute-start(bf16[2,64,4,128]{3,2,1,0:T(4,128)(2,1)S(1)} %get-tuple-element.2197), channel_id=1, source_target_pairs={{0,5},{1,4},{2,7},{3,6},{4,1},{5,0},{6,3},{7,2},{8,13},{9,12},{10,... | collective-permute-start | bytes 393224 | tf_op jit(solution)/shard_map/ppermute | solution.py:197
  1036.4 13.3 %collective-permute-start.6 = (bf16[2,64,4,128]{3,2,1,0:T(4,128)(2,1)S(1)}, bf16[2,64,4,128]{3,2,1,0:T(4,128)(2,1)S(1)}, u32[]{:S(2)}, u32[]{:S(2)}) collective-permute-start(bf16[2,64,4,128]{3,2,1,0:T(4,128)(2,1)S(1)} %get-tuple-element.2196), channel_id=1, source_target_pairs={{0,6},{1,7},{2,4},{3,5},{4,2},{5,3},{6,0},{7,1},{8,14},{9,15},{10,... | collective-permute-start | bytes 393224 | tf_op jit(solution)/shard_map/ppermute | solution.py:197
  1040.9 11.1 %collective-permute-start.7 = (bf16[2,64,4,128]{3,2,1,0:T(4,128)(2,1)S(1)}, bf16[2,64,4,128]{3,2,1,0:T(4,128)(2,1)S(1)}, u32[]{:S(2)}, u32[]{:S(2)}) collective-permute-start(bf16[2,64,4,128]{3,2,1,0:T(4,128)(2,1)S(1)} %get-tuple-element.2195), channel_id=1, source_target_pairs={{0,7},{1,6},{2,5},{3,4},{4,3},{5,2},{6,1},{7,0},{8,15},{9,14},{10,... | collective-permute-start | bytes 393224 | tf_op jit(solution)/shard_map/ppermute | solution.py:197
  1042.7 16.9 %collective-permute-start.8 = (bf16[2,64,4,128]{3,2,1,0:T(4,128)(2,1)S(1)}, bf16[2,64,4,128]{3,2,1,0:T(4,128)(2,1)S(1)}, u32[]{:S(2)}, u32[]{:S(2)}) collective-permute-start(bf16[2,64,4,128]{3,2,1,0:T(4,128)(2,1)S(1)} %get-tuple-element.2194), channel_id=1, source_target_pairs={{0,8},{1,9},{2,10},{3,11},{4,12},{5,13},{6,14},{7,15},{8,0},{9,1},... | collective-permute-start | bytes 393224 | tf_op jit(solution)/shard_map/ppermute | solution.py:197
  1042.9 21.9 %collective-permute-start.9 = (bf16[2,64,4,128]{3,2,1,0:T(4,128)(2,1)S(1)}, bf16[2,64,4,128]{3,2,1,0:T(4,128)(2,1)S(1)}, u32[]{:S(2)}, u32[]{:S(2)}) collective-permute-start(bf16[2,64,4,128]{3,2,1,0:T(4,128)(2,1)S(1)} %get-tuple-element.2193), channel_id=1, source_target_pairs={{0,9},{1,8},{2,11},{3,10},{4,13},{5,12},{6,15},{7,14},{8,1},{9,0},... | collective-permute-start | bytes 393224 | tf_op jit(solution)/shard_map/ppermute | solution.py:197
  1046.5 22.7 %collective-permute-start.10 = (bf16[2,64,4,128]{3,2,1,0:T(4,128)(2,1)S(1)}, bf16[2,64,4,128]{3,2,1,0:T(4,128)(2,1)S(1)}, u32[]{:S(2)}, u32[]{:S(2)}) collective-permute-start(bf16[2,64,4,128]{3,2,1,0:T(4,128)(2,1)S(1)} %get-tuple-element.2192), channel_id=1, source_target_pairs={{0,10},{1,11},{2,8},{3,9},{4,14},{5,15},{6,12},{7,13},{8,2},{9,3},... | collective-permute-start | bytes 393224 | tf_op jit(solution)/shard_map/ppermute | solution.py:197
  1049.7 23.9 %collective-permute-start.11 = (bf16[2,64,4,128]{3,2,1,0:T(4,128)(2,1)S(1)}, bf16[2,64,4,128]{3,2,1,0:T(4,128)(2,1)S(1)}, u32[]{:S(2)}, u32[]{:S(2)}) collective-permute-start(bf16[2,64,4,128]{3,2,1,0:T(4,128)(2,1)S(1)} %get-tuple-element.2191), channel_id=1, source_target_pairs={{0,11},{1,10},{2,9},{3,8},{4,15},{5,14},{6,13},{7,12},{8,3},{9,2},... | collective-permute-start | bytes 393224 | tf_op jit(solution)/shard_map/ppermute | solution.py:197
  1052.0 21.7 %collective-permute-start.12 = (bf16[2,64,4,128]{3,2,1,0:T(4,128)(2,1)S(1)}, bf16[2,64,4,128]{3,2,1,0:T(4,128)(2,1)S(1)}, u32[]{:S(2)}, u32[]{:S(2)}) collective-permute-start(bf16[2,64,4,128]{3,2,1,0:T(4,128)(2,1)S(1)} %get-tuple-element.2190), channel_id=1, source_target_pairs={{0,12},{1,13},{2,14},{3,15},{4,8},{5,9},{6,10},{7,11},{8,4},{9,5},... | collective-permute-start | bytes 393224 | tf_op jit(solution)/shard_map/ppermute | solution.py:197
  1059.6 14.3 %collective-permute-start.13 = (bf16[2,64,4,128]{3,2,1,0:T(4,128)(2,1)S(1)}, bf16[2,64,4,128]{3,2,1,0:T(4,128)(2,1)S(1)}, u32[]{:S(2)}, u32[]{:S(2)}) collective-permute-start(bf16[2,64,4,128]{3,2,1,0:T(4,128)(2,1)S(1)} %get-tuple-element.2189), channel_id=1, source_target_pairs={{0,13},{1,12},{2,15},{3,14},{4,9},{5,8},{6,11},{7,10},{8,5},{9,4},... | collective-permute-start | bytes 393224 | tf_op jit(solution)/shard_map/ppermute | solution.py:197
  1064.8 9.1 collective-permute-start.14
  1069.2 8.7 collective-permute-start.15
  (17 other events, 37.5 us)
